TPU v7x, 32 devices: a whole 2x2x4 slice. The times are simulated.
32 devices in a mesh: pages: 8 (over z, y), heads: 4 (over x, core).
Axes of the slice: x: 2, y: 2, z: 4, core: 2. Of those that a mesh axis runs over, the one named last changes fastest.
Arguments:
- x_in: bfloat16 [32, 561, 768], P('pages'), may hold values from -6 to 6
- cotangent: bfloat16 [32, 561, 768], P('pages'), may hold values from -6 to 6
- text_len: int32 [32], P('pages'), may hold values from 40 to 512, as said below
- coords: int32 [32, 3, 561], P('pages'), may hold values from 0 to 255
- grid_index: int32 [32, 49], P('pages'), may hold values from 0 to 48, each once within a row
- w_qkv: bfloat16 [768, 3, 768], P('pages', None, 'heads'), may hold values from -0.21875 to 0.21875
- b_qv: bfloat16 [2, 768], P(None, ('heads', 'pages')), may hold values from -3 to 3
- w_out: bfloat16 [768, 768], P(('heads', 'pages')), may hold values from -0.875 to 0.875
- w_up: bfloat16 [768, 3072], P('pages', 'heads'), may hold values from -0.21875 to 0.21875
- b_up: bfloat16 [3072], P(('heads', 'pages')), may hold values from -3 to 3
- w_down: bfloat16 [3072, 768], P(('heads', 'pages')), may hold values from -0.109375 to 0.109375
- rel_bias: bfloat16 [3, 128, 12], P(None, 'pages', 'heads'), may hold values from -3 to 3
- conv_w: bfloat16 [18, 768], P(None, ('pages', 'heads')), may hold values from -2 to 2
- biases: bfloat16 [6, 768], P(None, ('pages', 'heads')), may hold values from -2 to 2
- gains: bfloat16 [2, 768], P(None, ('pages', 'heads')), may hold values from 0.5 to 1.5
Outputs:
- out: bfloat16 [32, 561, 768], P('pages')
- grad_x: float32 [32, 561, 768], P('pages')
- grad_w_qkv: float32 [768, 3, 768], P('pages', None, 'heads')
- grad_b_qv: float32 [2, 768], P(None, ('heads', 'pages'))
- grad_w_out: float32 [768, 768], P(('heads', 'pages'))
- grad_w_up: float32 [768, 3072], P('pages', 'heads')
- grad_b_up: float32 [3072], P(('heads', 'pages'))
- grad_w_down: float32 [3072, 768], P(('heads', 'pages'))
- grad_rel_bias: float32 [3, 128, 12], P(None, 'pages', 'heads')
- grad_conv_w: float32 [18, 768], P(None, ('pages', 'heads'))
- grad_biases: float32 [6, 768], P(None, ('pages', 'heads'))
- grad_gains: float32 [2, 768], P(None, ('pages', 'heads'))
Inputs may be any that keep to these rules, and one draw needn't show every extreme that they name: `text_len`: every page has at most 512 text tokens, and some page has exactly 512. `grid_index`: each page's row names every cell of the grid once.
All inputs are finite; a program needn't handle non-finite values.
Results may differ from a plain program's by a relative error of at most 0.024.
The roundings to bfloat16 on the way count: a program that leaves them out, or rounds other values in their place, can miss the bound.
Values may be sent and summed in bfloat16 or wider, within the bound.
A program may use at most 192 MiB of HBM per device.

v0:
```python
import jax
import jax.numpy as jnp
from jax import lax
from jax.sharding import PartitionSpec as P

HD = 64
TXT = 512
GRID = 7
NB = 128


HIGHEST = lax.Precision.HIGHEST
EPSILON = 1e-05


def layer_norm(values, gain_row, shift_row):
    average = jnp.mean(values, -1, keepdims=True)
    centred = values - average
    variance = jnp.mean(centred * centred, -1, keepdims=True)
    return centred * lax.rsqrt(variance + EPSILON) * gain_row + shift_row


def valid_slots(text_len, seq_len):
    positions = jnp.arange(seq_len, dtype=jnp.int32)
    return jnp.logical_or(positions[None, :] < text_len[:, None], positions[None, :] >= TXT)


def offset_table():
    span_ids = jnp.arange(2 * NB, dtype=jnp.int32)
    offsets = span_ids[None, :] - span_ids[:, None]
    bucket_of = jnp.clip(offsets, -(NB // 2), NB // 2 - 1) + NB // 2
    return (bucket_of[:, :, None] == jnp.arange(NB, dtype=jnp.int32)[None, None, :]).astype(
        jnp.bfloat16
    )


def placed_of(coords_page):
    return (coords_page[:, :, None] == jnp.arange(2 * NB, dtype=jnp.int32)[None, None, :]).astype(
        jnp.bfloat16
    )


def toeplitz_of(offsets_map, rel_table):
    return jnp.einsum(
        "abk,ckh->chab", offsets_map, rel_table, preferred_element_type=jnp.float32
    ).astype(jnp.bfloat16)


def dcpe(field, valid, grid_index, kernel, first_bias, second_bias):
    page_count = field.shape[0]
    model_width = field.shape[-1]
    cell_count = GRID * GRID
    masked = field * valid[:, :, None].astype(field.dtype)
    text_part = masked[:, :TXT]
    padded = jnp.pad(text_part, ((0, 0), (3, 3), (0, 0)))
    text_out = jnp.zeros_like(text_part) + first_bias
    for spacing in range(1, 4):
        for offset_no in range(3):
            shift_at = 3 + (offset_no - 1) * spacing
            text_out = (
                text_out
                + kernel[3 * (spacing - 1) + offset_no] * padded[:, shift_at : shift_at + TXT]
            )
    placement = (
        grid_index[:, :, None] == jnp.arange(cell_count, dtype=jnp.int32)[None, None, :]
    ).astype(field.dtype)
    on_grid = jnp.einsum("psc,psd->pcd", placement, masked[:, TXT:], precision=HIGHEST)
    on_grid = jnp.pad(
        on_grid.reshape(page_count, GRID, GRID, model_width), ((0, 0), (1, 1), (1, 1), (0, 0))
    )
    grid_out = jnp.zeros((page_count, GRID, GRID, model_width), field.dtype) + second_bias
    for row_no in range(3):
        for col_no in range(3):
            grid_out = (
                grid_out
                + kernel[9 + 3 * row_no + col_no]
                * on_grid[:, row_no : row_no + GRID, col_no : col_no + GRID]
            )
    patch_out = jnp.einsum(
        "psc,pcd->psd",
        placement,
        grid_out.reshape(page_count, cell_count, model_width),
        precision=HIGHEST,
    )
    return jnp.concatenate([text_out, patch_out], 1)


def page_scores(queries, key_rows, valid_page, placed, toeplitz):
    products = (
        jnp.einsum("ihd,jhd->hij", queries, key_rows, preferred_element_type=jnp.float32) * 0.125
    )
    left_part = jnp.einsum(
        "cia,chab->chib", placed, toeplitz, preferred_element_type=jnp.float32
    ).astype(jnp.bfloat16)
    rel_terms = jnp.einsum("chib,cjb->hij", left_part, placed, preferred_element_type=jnp.float32)
    return jnp.where(valid_page[None, None, :], products + rel_terms, -1e30)


def attend_page(queries, key_rows, value_rows, valid_page, coords_page, toeplitz):
    scores = page_scores(queries, key_rows, valid_page, placed_of(coords_page), toeplitz)
    highest = jnp.max(scores, -1, keepdims=True)
    weights = jnp.exp(scores - highest)
    norm_total = jnp.sum(weights, -1, keepdims=True)
    probs = (weights / norm_total).astype(jnp.bfloat16)
    mixed = jnp.einsum(
        "hij,jhd->ihd", probs, value_rows, preferred_element_type=jnp.float32
    ).astype(jnp.bfloat16)
    return (mixed, (highest + jnp.log(norm_total))[..., 0])


def back_page(queries, key_rows, value_rows, valid_page, coords_page, toeplitz, log_total, d_mixed):
    placed = placed_of(coords_page)
    scores = page_scores(queries, key_rows, valid_page, placed, toeplitz)
    probs = jnp.exp(scores - log_total[..., None])
    d_probs = jnp.einsum("ihd,jhd->hij", d_mixed, value_rows, preferred_element_type=jnp.float32)
    centre = jnp.sum(probs * d_probs, -1, keepdims=True)
    d_scores = (probs * (d_probs - centre)).astype(jnp.bfloat16)
    d_query = (
        jnp.einsum("hij,jhd->ihd", d_scores, key_rows, preferred_element_type=jnp.float32) * 0.125
    ).astype(jnp.bfloat16)
    d_key = (
        jnp.einsum("hij,ihd->jhd", d_scores, queries, preferred_element_type=jnp.float32) * 0.125
    ).astype(jnp.bfloat16)
    d_value = jnp.einsum(
        "hij,ihd->jhd", probs.astype(jnp.bfloat16), d_mixed, preferred_element_type=jnp.float32
    ).astype(jnp.bfloat16)
    spread = jnp.einsum("cia,hij->chaj", placed, d_scores, preferred_element_type=jnp.float32)
    table_grad = jnp.einsum("chaj,cjb->chab", spread, placed.astype(jnp.float32), precision=HIGHEST)
    return (d_query, d_key, d_value, table_grad)


def local(
    x_in,
    cotangent,
    text_len,
    coords,
    grid_index,
    w_qkv,
    b_qv,
    w_out,
    w_up,
    b_up,
    w_down,
    rel_bias,
    conv_w,
    biases,
    gains,
):
    f32 = jnp.float32
    bf16 = jnp.bfloat16
    head_id = lax.axis_index("heads")
    local_share = conv_w.shape[1]
    layer = (
        lax.all_gather(w_qkv, "pages", axis=0, tiled=True),
        lax.all_gather(b_qv, "pages", axis=1, tiled=True),
        lax.all_gather(w_out, "pages", axis=0, tiled=True),
        lax.all_gather(w_up, "pages", axis=0, tiled=True),
        lax.all_gather(b_up, "pages", axis=0, tiled=True),
        lax.all_gather(w_down, "pages", axis=0, tiled=True),
        lax.all_gather(rel_bias, "pages", axis=1, tiled=True),
    )
    shared = (
        lax.all_gather(conv_w, ("pages", "heads"), axis=1, tiled=True),
        lax.all_gather(biases, ("pages", "heads"), axis=1, tiled=True),
        lax.all_gather(gains, ("pages", "heads"), axis=1, tiled=True),
    )
    page_count, seq_len, model_width = x_in.shape
    heads_here = layer[6].shape[2]
    col_count = heads_here * HD
    row_count = page_count * seq_len
    qkv_flat = layer[0].reshape(model_width, 3 * col_count)
    out_full = layer[2]
    up_full = layer[3]
    down_full = layer[5]
    offsets_map = offset_table()
    toeplitz = toeplitz_of(offsets_map, layer[6])
    kernel_float = shared[0].astype(f32)
    bias_float = shared[1].astype(f32)
    gain_float = shared[2].astype(f32)
    valid = valid_slots(text_len, seq_len)

    def conv_part(values, kernel, first_bias, second_bias):
        return dcpe(values, valid, grid_index, kernel, first_bias, second_bias)

    field = x_in.astype(f32)
    h_one = field + conv_part(field, kernel_float, bias_float[0], bias_float[1])
    h_one_rows = h_one.reshape(row_count, model_width)
    act_in = h_one_rows.astype(bf16)
    qkv_bias = jnp.concatenate(
        [layer[1][0].astype(f32), jnp.zeros((col_count,), f32), layer[1][1].astype(f32)]
    )
    projected = (jnp.dot(act_in, qkv_flat, preferred_element_type=f32) + qkv_bias).astype(bf16)
    split_shape = (page_count, seq_len, heads_here, HD)
    queries = projected[:, :col_count].reshape(split_shape)
    key_rows = projected[:, col_count : 2 * col_count].reshape(split_shape)
    value_rows = projected[:, 2 * col_count :].reshape(split_shape)
    heads_out, log_total = lax.map(
        lambda entry: attend_page(entry[0], entry[1], entry[2], entry[3], entry[4], toeplitz),
        (queries, key_rows, value_rows, valid, coords),
    )
    mixed = heads_out.reshape(row_count, col_count)
    attn = (
        lax.psum(
            jnp.dot(mixed, out_full, preferred_element_type=f32).astype(jnp.bfloat16), "heads"
        ).astype(jnp.float32)
        + bias_float[2]
    )
    h_two_pre = h_one_rows + attn
    h_two = layer_norm(h_two_pre, gain_float[0], bias_float[3])
    ffn_in = h_two.astype(bf16)
    hidden = jnp.dot(ffn_in, up_full, preferred_element_type=f32) + layer[4].astype(f32)
    activated = jax.nn.gelu(hidden, approximate=False).astype(bf16)
    ffn = (
        lax.psum(
            jnp.dot(activated, down_full, preferred_element_type=f32).astype(jnp.bfloat16), "heads"
        ).astype(jnp.float32)
        + bias_float[4]
    )
    summed = h_two + ffn
    result = layer_norm(summed, gain_float[1], bias_float[5])
    again_layer = (
        lax.all_gather(w_qkv, "pages", axis=0, tiled=True),
        lax.all_gather(w_out, "pages", axis=0, tiled=True),
        lax.all_gather(w_up, "pages", axis=0, tiled=True),
        lax.all_gather(w_down, "pages", axis=0, tiled=True),
        lax.all_gather(rel_bias, "pages", axis=1, tiled=True),
    )
    shared_again = (
        lax.all_gather(conv_w, ("pages", "heads"), axis=1, tiled=True),
        lax.all_gather(gains, ("pages", "heads"), axis=1, tiled=True),
    )
    back_qkv = again_layer[0].reshape(model_width, 3 * col_count)
    back_out = again_layer[1]
    back_up = again_layer[2]
    back_down = again_layer[3]
    back_toeplitz = toeplitz_of(offsets_map, again_layer[4])
    back_kernel = shared_again[0].astype(f32)
    back_gain = shared_again[1].astype(f32)
    d_result = cotangent.reshape(row_count, model_width).astype(f32)
    norm_two_back = jax.vjp(layer_norm, summed, back_gain[1], bias_float[5])[1]
    d_sum, d_gain_two, d_shift_two = norm_two_back(d_result)
    d_ffn = d_sum.astype(bf16)
    grad_bias_down = jnp.sum(d_ffn.astype(f32), 0)
    grad_down = jnp.einsum("nf,nd->fd", activated, d_ffn, preferred_element_type=f32)
    d_act = jnp.einsum("nd,fd->nf", d_ffn, back_down, preferred_element_type=f32)
    gelu_back = jax.vjp(lambda inner: jax.nn.gelu(inner, approximate=False), hidden)[1]
    d_hidden = gelu_back(d_act)[0].astype(bf16)
    grad_up_bias = jnp.sum(d_hidden.astype(f32), 0)
    grad_up = jnp.einsum("nd,nf->df", ffn_in, d_hidden, preferred_element_type=f32)
    d_two = d_sum + lax.psum(
        jnp.einsum("nf,df->nd", d_hidden, back_up, preferred_element_type=f32).astype(jnp.bfloat16),
        "heads",
    ).astype(jnp.float32)
    norm_one_back = jax.vjp(layer_norm, h_two_pre, back_gain[0], bias_float[3])[1]
    d_pre, d_gain_one, d_shift_one = norm_one_back(d_two)
    d_attn = d_pre.astype(bf16)
    grad_out_bias = jnp.sum(d_attn.astype(f32), 0)
    grad_out = jnp.einsum("nc,nd->cd", mixed, d_attn, preferred_element_type=f32)
    d_mixed = jnp.einsum("nd,cd->nc", d_attn, back_out, preferred_element_type=f32).astype(bf16)

    def back_step(table_total, entry):
        d_query, d_key, d_value, table_grad = back_page(
            entry[0], entry[1], entry[2], entry[3], entry[4], back_toeplitz, entry[5], entry[6]
        )
        return (table_total + table_grad, (d_query, d_key, d_value))

    table_init = jnp.zeros((3, heads_here, 2 * NB, 2 * NB), f32)
    table_total, pieces = lax.scan(
        back_step,
        table_init,
        (queries, key_rows, value_rows, valid, coords, log_total, d_mixed.reshape(split_shape)),
    )
    grad_rel = jnp.einsum("abk,chab->ckh", offsets_map.astype(f32), table_total, precision=HIGHEST)
    d_query_rows = pieces[0].reshape(row_count, col_count)
    d_value_rows = pieces[2].reshape(row_count, col_count)
    d_proj = jnp.concatenate(
        [d_query_rows, pieces[1].reshape(row_count, col_count), d_value_rows], -1
    )
    grad_qkv = jnp.einsum("nd,ne->de", act_in, d_proj, preferred_element_type=f32).reshape(
        model_width, 3, col_count
    )
    grad_qv_bias = jnp.stack(
        [jnp.sum(d_query_rows.astype(f32), 0), jnp.sum(d_value_rows.astype(f32), 0)]
    )
    d_one = d_pre + lax.psum(
        jnp.einsum("ne,de->nd", d_proj, back_qkv, preferred_element_type=f32).astype(jnp.bfloat16),
        "heads",
    ).astype(jnp.float32)
    d_one_pages = d_one.reshape(page_count, seq_len, model_width)
    conv_back = jax.vjp(conv_part, field, back_kernel, bias_float[0], bias_float[1])[1]
    d_field, grad_kernel, d_first, d_second = conv_back(d_one_pages)
    grad_x = d_one_pages + d_field
    grad_bias_rows = jnp.stack(
        [d_first, d_second, grad_out_bias, d_shift_one, grad_bias_down, d_shift_two]
    )
    grad_gain_rows = jnp.stack([d_gain_one, d_gain_two])
    scattered = (
        lax.psum_scatter(grad_qkv, "pages", scatter_dimension=0, tiled=True),
        lax.psum_scatter(grad_qv_bias, "pages", scatter_dimension=1, tiled=True),
        lax.psum_scatter(grad_out, "pages", scatter_dimension=0, tiled=True),
        lax.psum_scatter(grad_up, "pages", scatter_dimension=0, tiled=True),
        lax.psum_scatter(grad_up_bias, "pages", scatter_dimension=0, tiled=True),
        lax.psum_scatter(grad_down, "pages", scatter_dimension=0, tiled=True),
        lax.psum_scatter(grad_rel, "pages", scatter_dimension=1, tiled=True),
        lax.psum_scatter(grad_kernel, "pages", scatter_dimension=1, tiled=True),
        lax.psum_scatter(grad_bias_rows, "pages", scatter_dimension=1, tiled=True),
        lax.psum_scatter(grad_gain_rows, "pages", scatter_dimension=1, tiled=True),
    )

    def own_share(values):
        return lax.dynamic_slice_in_dim(values, head_id * local_share, local_share, 1)

    return (
        result.reshape(page_count, seq_len, model_width).astype(bf16),
        grad_x,
        scattered[0],
        scattered[1],
        scattered[2],
        scattered[3],
        scattered[4],
        scattered[5],
        scattered[6],
        own_share(scattered[7]),
        own_share(scattered[8]),
        own_share(scattered[9]),
    )


def solution(mesh):
    return jax.shard_map(
        local,
        mesh=mesh,
        in_specs=(
            P("pages", None, None),
            P("pages", None, None),
            P("pages"),
            P("pages", None, None),
            P("pages", None),
            P("pages", None, "heads"),
            P(None, ("heads", "pages")),
            P(("heads", "pages"), None),
            P("pages", "heads"),
            P(("heads", "pages")),
            P(("heads", "pages"), None),
            P(None, "pages", "heads"),
            P(None, ("pages", "heads")),
            P(None, ("pages", "heads")),
            P(None, ("pages", "heads")),
        ),
        out_specs=(
            P("pages", None, None),
            P("pages", None, None),
            P("pages", None, "heads"),
            P(None, ("heads", "pages")),
            P(("heads", "pages"), None),
            P("pages", "heads"),
            P(("heads", "pages")),
            P(("heads", "pages"), None),
            P(None, "pages", "heads"),
            P(None, ("pages", "heads")),
            P(None, ("pages", "heads")),
            P(None, ("pages", "heads")),
        ),
        check_vma=False,
    )
```

profile of v0, /device:TPU:9, one launch (start us, length us, event | category | flops | bytes accessed | tf_op | source)
XLA Modules:
  0.0 1385.1 jit_solution(6114857692817765726)
XLA Ops:
  8.2 14.4 %all-gather.1 = bf16[8,24,2]{1,2,0:T(2,128)(2,1)S(1)} all-gather(bf16[1,24,2]{1,2,0:T(2,128)(2,1)} %bitcast.319), channel_id=1, replica_groups=mesh['pages'=8,'heads'=4] {'pages'}, dimensions={0}, use_global_device_ids=true | all-gather | bytes 864 | tf_op jit(solution)/shard_map/all_gather | solution.py:155
  25.0 38.9 %all-gather = bf16[32,24,6]{1,2,0:T(8,128)(2,1)S(1)} all-gather(bf16[1,24,6]{1,2,0:T(8,128)(2,1)} %bitcast.318), channel_id=1, replica_groups=mesh['pages'=8,'heads'=4] {'pages','heads'}, dimensions={0}, use_global_device_ids=true | all-gather | bytes 9504 | tf_op jit(solution)/shard_map/all_gather | solution.py:164
  64.9 27.7 %all_gather.41 = bf16[3,128,3]{2,0,1:T(4,128)(2,1)S(1)} all-gather(bf16[3,16,3]{2,0,1:T(4,128)(2,1)S(1)} %copy.173), channel_id=1, replica_groups=mesh['pages'=8,'heads'=4] {'pages'}, dimensions={1}, use_global_device_ids=true | all-gather | bytes 2592 | tf_op jit(solution)/shard_map/all_gather | solution.py:160
  92.7 40.1 %all_gather.38 = bf16[18,768]{0,1:T(8,128)(2,1)S(1)} all-gather(bf16[18,24]{0,1:T(8,128)(2,1)S(1)} %copy.166), channel_id=1, replica_groups=mesh['pages'=8,'heads'=4] {'pages','heads'}, dimensions={1}, use_global_device_ids=true | all-gather | bytes 28512 | tf_op jit(solution)/shard_map/all_gather | solution.py:163
  136.8 30.1 %all_gather.42 = bf16[192,768]{1,0:T(8,128)(2,1)} all-gather(bf16[24,768]{1,0:T(8,128)(2,1)S(1)} %copy-done.66), channel_id=1, replica_groups=mesh['pages'=8,'heads'=4] {'pages'}, dimensions={0}, use_global_device_ids=true | all-gather | bytes 331776 | tf_op jit(solution)/shard_map/all_gather | solution.py:156
  166.9 34.3 %all_gather.39 = bf16[768,3,192]{2,1,0:T(4,128)(2,1)S(1)} all-gather(bf16[96,3,192]{2,1,0:T(4,128)(2,1)S(1)} %copy.170), channel_id=1, replica_groups=mesh['pages'=8,'heads'=4] {'pages'}, dimensions={0}, use_global_device_ids=true | all-gather | bytes 995328 | tf_op jit(solution)/shard_map/all_gather | solution.py:154
  203.3 14.9 %fusion.106 = bf16[3,3,256,256]{3,1,0,2:T(4,128)(2,1)S(1)} fusion(s32[256,256]{1,0:T(8,128)S(1)} %clamp_add_fusion, bf16[3,128,3]{1,2,0:T(4,128)(2,1)S(1)} %copy.174), kind=kOutput, calls=%fused_computation.179 | convolution fusion | flops 159973376 | bytes 1444096 | tf_op jit(solution)/shard_map/abk,ckh->chab/dot_general | solution.py:44
  256.5 48.7 %while.29 = (s32[]{:T(128)}, bf16[4,561,3,64]{1,3,2,0:T(8,128)(2,1)}, f32[4,3,561]{2,1,0:T(4,128)}, bf16[4,561,3,64]{1,3,2,0:T(8,128)(2,1)S(1)}, pred[4,561]{1,0...) while((s32[]{:T(128)}, ...), condition=%wide.region_3.4_spmd, body=%wide.region_0.3_spmd.sunk | while | flops 2364480512 | bytes 21720428 | solution.py:197
  316.9 15.9 %all-reduce.40 = bf16[768]{0:T(1024)(128)(2,1)S(1)} all-reduce(bf16[768]{0:T(1024)(128)(2,1)S(1)} %dynamic-update-slice), channel_id=1, replica_groups=mesh['pages'=8,'heads'=4] {'pages'}, use_global_device_ids=true, to_apply=%add.40 | all-reduce | flops 768 | bytes 3072
  332.8 47.2 %all-gather.2 = bf16[32,24,2]{1,2,0:T(2,128)(2,1)S(1)} all-gather(bf16[1,24,2]{1,2,0:T(2,128)(2,1)S(1)} %bitcast.320), channel_id=1, replica_groups=mesh['pages'=8,'heads'=4] {'pages','heads'}, dimensions={0}, use_global_device_ids=true | all-gather | bytes 3168 | tf_op jit(solution)/shard_map/all_gather | solution.py:165
  407.1 21.7 %multiply_convert_fusion.1 = (bf16[2244,768]{1,0:T(8,128)(2,1)}, f32[2244,768]{1,0:T(8,128)}, f32[2244,768]{1,0:T(8,128)}) fusion(f32[768]{0:T(1024)S(1)} %convert_element_type.206, bf16[2244,768]{1,0:T(8,128)(2,1)S(1)} %fusion.101, bf16[768,768]{1,0:T(8,128)(2,1)} %all-gather.6.cloned.1.call-done), kind=kOutput, calls=%fused_computation.111 | convolution fusion | flops 2760873984 | bytes 21863424 | tf_op jit(solution)/shard_map/dot_general | solution.py:211
  447.0 62.7 %all-reduce.51.cloned.1.call-done = bf16[2244,768]{1,0:T(8,128)(2,1)} async-done(((bf16[2244,768]{1,0:T(8,128)(2,1)}), bf16[2244,768]{1,0:T(8,128)(2,1)}) %all-reduce.51.cloned.1.call-update) | async-done | bytes 3446800 | tf_op jit(solution)/shard_map/psum | solution.py:214
  544.7 73.7 %all-reduce.53.cloned.1.call-done = bf16[2244,768]{1,0:T(8,128)(2,1)} async-done(((bf16[2244,768]{1,0:T(8,128)(2,1)}), bf16[2244,768]{1,0:T(8,128)(2,1)}) %all-reduce.53.cloned.1.call-update) | async-done | bytes 3446800 | tf_op jit(solution)/shard_map/psum | solution.py:250
  651.8 129.4 %while.30 = (s32[]{:T(128)}, f32[3,3,256,256]{3,2,1,0:T(8,128)S(1)}, bf16[4,561,3,64]{1,3,2,0:T(8,128)(2,1)}, bf16[4,561,3,64]{1,3,2,0:T(8,128)(2,1)}, bf16[4,56...) while((s32[]{:T(128)}, ...), condition=%wide.region_17.18_spmd.clone, body=%wide.region_15.17_spmd.clone.sunk | while | flops 8151384576 | bytes 71091712 | solution.py:268
  807.4 30.7 %fusion.109 = f32[3,128,3]{1,2,0:T(4,128)S(1)} fusion(s32[256,256]{1,0:T(8,128)S(1)} %copy-done.36, f32[3,3,256,256]{3,2,1,0:T(8,128)S(1)} %get-tuple-element.135), kind=kOutput, calls=%fused_computation.180 | convolution fusion | flops 914358272 | bytes 2626048 | tf_op jit(solution)/shard_map/abk,chab->ckh/dot_general | solution.py:273
  841.3 35.2 %all-reduce.55.cloned.1.call-done = bf16[2244,768]{1,0:T(8,128)(2,1)} async-done(((bf16[2244,768]{1,0:T(8,128)(2,1)}), bf16[2244,768]{1,0:T(8,128)(2,1)}) %all-reduce.55.cloned.1.call-update) | async-done | bytes 3446800 | tf_op jit(solution)/shard_map/psum | solution.py:285
  893.5 29.3 %multiply_reduce_fusion.13 = (f32[768]{0:T(1024)}, f32[768]{0:T(1024)}, f32[768]{0:T(1024)S(1)}, f32[768]{0:T(1024)S(1)}, f32[768]{0:T(1024)S(1)}, /*index=5*/f3...) fusion(f32[4,512,768]{2,1,0:T(8,128)} %copy-done.4, ...), kind=kLoop, calls=%fused_computation.143 | loop fusion | flops 31451136 | bytes 50371584 | tf_op jit(solution)/shard_map/transpose(jvp())/reduce_sum | solution.py:62
  968.5 15.5 %all-reduce.43 = (f32[2,192]{1,0:T(2,128)S(1)}, f32[768]{0:T(1024)S(1)}) all-reduce(f32[2,192]{1,0:T(2,128)S(1)} %pad_maximum_fusion.2, f32[768]{0:T(1024)S(1)} %copy-done.88), channel_id=3, replica_groups=mesh['pages'=8,'heads'=4] {'pages'}, use_global_device_ids=true, to_apply=%region_22.23.clone | all-reduce | flops 1152 | bytes 9216
  1011.6 16.6 %pad_add_fusion.1 = f32[4,512,768]{2,1,0:T(8,128)} fusion(f32[4,512,768]{2,1,0:T(8,128)} %get-tuple-element.465, f32[4,512,768]{2,1,0:T(8,128)} %get-tuple-element.466, f32[4,512,768]{2,1,0:T(8,128)} %get-tuple-element.473, f32[4,512,768]{2,1,0:T(8,128)} %get-tuple-element.472, f32[4,512,768]{2,1,0:T(8,128)} %get-tuple-element.471, ...), kind=kLoop, calls=%fused_computation.131 | loop fusion | flops 9437184 | bytes 50331648 | tf_op jit(solution)/shard_map/transpose(jvp())/add_any | solution.py:62
  1040.5 52.8 %reduce-scatter.28.cloned.1.call-done = f32[96,18]{1,0:T(8,128)} async-done(((f32[768,18]{1,0:T(8,128)}), f32[96,18]{1,0:T(8,128)}) %reduce-scatter.28.cloned.1.call-update) | async-done | bytes 6928
  1094.6 64.0 %reduce-scatter.20.cloned.1.call-done = f32[24,768]{1,0:T(8,128)} async-done(((f32[192,768]{1,0:T(8,128)}), f32[24,768]{1,0:T(8,128)}) %reduce-scatter.20.cloned.1.call-update) | async-done | bytes 73744 | tf_op jit(solution)/shard_map/reduce_scatter | solution.py:300
  1158.7 72.8 %reduce-scatter.22.cloned.1.call-done = f32[96,768]{1,0:T(8,128)} async-done(((f32[768,768]{1,0:T(8,128)}), f32[96,768]{1,0:T(8,128)}) %reduce-scatter.22.cloned.1.call-update) | async-done | bytes 294928 | tf_op jit(solution)/shard_map/reduce_scatter | solution.py:301
  1231.5 73.1 %reduce-scatter.24.cloned.1.call-done = f32[96,768]{1,0:T(8,128)} async-done(((f32[768,768]{1,0:T(8,128)}), f32[96,768]{1,0:T(8,128)}) %reduce-scatter.24.cloned.1.call-update) | async-done | bytes 294928 | tf_op jit(solution)/shard_map/reduce_scatter | solution.py:303
  1304.6 73.2 %reduce-scatter.18.cloned.1.call-done = f32[96,3,192]{2,0,1:T(8,128)} async-done(((f32[768,3,192]{2,0,1:T(8,128)}), f32[96,3,192]{2,0,1:T(8,128)}) %reduce-scatter.18.cloned.1.call-update) | async-done | bytes 221200 | tf_op jit(solution)/shard_map/reduce_scatter | solution.py:298
  (501 shorter events, 480.4 us)
Async XLA Ops:
  8.0 128.5 %copy-start.37 = (bf16[96,3,192]{2,0,1:T(8,128)(2,1)S(1)}, bf16[96,3,192]{2,0,1:T(8,128)(2,1)}, u32[]{:S(2)}) copy-start(bf16[96,3,192]{2,0,1:T(8,128)(2,1)} %param.24) | copy-start | bytes 331780
  8.0 128.8 %copy-start.66 = (bf16[24,768]{1,0:T(8,128)(2,1)S(1)}, bf16[24,768]{1,0:T(8,128)(2,1)}, u32[]{:S(2)}) copy-start(bf16[24,768]{1,0:T(8,128)(2,1)} %param.26) | copy-start | bytes 110596
  8.0 389.8 %all-reduce.49.cloned.1.call-start = ((), (), s32[]{:S(2)}) async-start(), calls=%async_computation.8 | async-start | bytes 6905856 | tf_op jit(solution)/shard_map/psum | solution.py:203
  8.1 195.2 %copy-start.35 = (s32[256,256]{1,0:T(8,128)}, s32[256,256]{1,0:T(8,128)S(1)}, u32[]{:S(2)}) copy-start(s32[256,256]{1,0:T(8,128)S(1)} %clamp_add_fusion) | copy-start | bytes 786436
  136.6 89.3 %copy-start.40 = (f32[768]{0:T(1024)}, f32[768]{0:T(1024)S(1)}, u32[]{:S(2)}) copy-start(f32[768]{0:T(1024)S(1)} %get-tuple-element.381) | copy-start | bytes 9220
  136.6 89.3 %copy-start.42 = (f32[768]{0:T(1024)}, f32[768]{0:T(1024)S(1)}, u32[]{:S(2)}) copy-start(f32[768]{0:T(1024)S(1)} %get-tuple-element.385) | copy-start | bytes 9220
  136.6 89.3 %copy-start.44 = (f32[768]{0:T(1024)}, f32[768]{0:T(1024)S(1)}, u32[]{:S(2)}) copy-start(f32[768]{0:T(1024)S(1)} %get-tuple-element.386) | copy-start | bytes 9220
  136.6 89.3 %copy-start.46 = (f32[768]{0:T(1024)}, f32[768]{0:T(1024)S(1)}, u32[]{:S(2)}) copy-start(f32[768]{0:T(1024)S(1)} %get-tuple-element.387) | copy-start | bytes 9220
  136.6 89.3 %copy-start.67 = (f32[768]{0:T(1024)}, f32[768]{0:T(1024)S(1)}, u32[]{:S(2)}) copy-start(f32[768]{0:T(1024)S(1)} %get-tuple-element.371) | copy-start | bytes 9220
  136.6 89.3 %copy-start.69 = (f32[768]{0:T(1024)}, f32[768]{0:T(1024)S(1)}, u32[]{:S(2)}) copy-start(f32[768]{0:T(1024)S(1)} %get-tuple-element.382) | copy-start | bytes 9220
  136.6 89.3 %copy-start.71 = (f32[768]{0:T(1024)}, f32[768]{0:T(1024)S(1)}, u32[]{:S(2)}) copy-start(f32[768]{0:T(1024)S(1)} %get-tuple-element.383) | copy-start | bytes 9220
  314.2 92.9 %all-gather.6.cloned.1.call-start = ((), (), s32[]{:S(2)}) async-start(), calls=%async_computation.9 | async-start | bytes 1327104 | tf_op jit(solution)/shard_map/all_gather | solution.py:157
  314.7 114.0 %all-gather.8.cloned.1.call-start = ((), (), s32[]{:S(2)}) async-start(), calls=%async_computation.10 | async-start | bytes 1327104 | tf_op jit(solution)/shard_map/all_gather | solution.py:159
  315.3 194.4 %all-reduce.51.cloned.1.call-start = ((), (), s32[]{:S(2)}) async-start(), calls=%async_computation.11 | async-start | bytes 6905856 | tf_op jit(solution)/shard_map/psum | solution.py:214
  435.9 182.6 %all-reduce.53.cloned.1.call-start = ((), (), s32[]{:S(2)}) async-start(), calls=%async_computation.12 | async-start | bytes 6905856 | tf_op jit(solution)/shard_map/psum | solution.py:250
  544.7 331.8 %all-reduce.55.cloned.1.call-start = ((), (), s32[]{:S(2)}) async-start(), calls=%async_computation.13 | async-start | bytes 6905856 | tf_op jit(solution)/shard_map/psum | solution.py:285
  802.7 190.0 %reduce-scatter.26.cloned.1.call-start = ((), (), s32[]{:S(2)}) async-start(), calls=%async_computation.18 | async-start | bytes 73728
  839.0 155.2 %reduce-scatter.32.cloned.1.call-start = ((), (), s32[]{:S(2)}) async-start(), calls=%async_computation.21 | async-start | bytes 442368
  841.3 197.9 %reduce-scatter.30.cloned.1.call-start = ((), (), s32[]{:S(2)}) async-start(), calls=%async_computation.20 | async-start | bytes 442368
  938.0 155.3 %reduce-scatter.28.cloned.1.call-start = ((), (), s32[]{:S(2)}) async-start(), calls=%async_computation.19 | async-start | bytes 442368
  939.9 218.8 %reduce-scatter.20.cloned.1.call-start = ((), (), s32[]{:S(2)}) async-start(), calls=%async_computation.15 | async-start | bytes 663552 | tf_op jit(solution)/shard_map/reduce_scatter | solution.py:300
  942.9 288.6 %reduce-scatter.22.cloned.1.call-start = ((), (), s32[]{:S(2)}) async-start(), calls=%async_computation.16 | async-start | bytes 2654208 | tf_op jit(solution)/shard_map/reduce_scatter | solution.py:301
  950.3 354.2 %reduce-scatter.24.cloned.1.call-start = ((), (), s32[]{:S(2)}) async-start(), calls=%async_computation.17 | async-start | bytes 2654208 | tf_op jit(solution)/shard_map/reduce_scatter | solution.py:303
  957.9 419.9 %reduce-scatter.18.cloned.1.call-start = ((), (), s32[]{:S(2)}) async-start(), calls=%async_computation.14 | async-start | bytes 2654208 | tf_op jit(solution)/shard_map/reduce_scatter | solution.py:298
  (102 other events, 2137.4 us)
Sparse Core Ops, SparseCore 0:
  314.2 83.5 all-reduce.48
  436.0 73.6 all-reduce.50
  544.8 73.6 all-reduce.52
  802.8 73.6 all-reduce.54
Sparse Core Ops, SparseCore 1:
  316.8 49.4 all-gather.5
  368.3 39.5 all-gather.7
  839.1 60.5 reduce-scatter.25
  903.0 61.1 reduce-scatter.31
  967.5 61.2 reduce-scatter.29
  1032.0 61.2 reduce-scatter.27
  1097.0 61.6 reduce-scatter.19
  1162.6 68.8 reduce-scatter.21
  1235.4 69.1 reduce-scatter.23
  1308.6 69.1 reduce-scatter.17
where the time goes:
time: 1400 us; the launch traced here: 1390 us
  waiting for transfers between devices  520 us (37%)
  matrix products  297 us (21%)
  blocking collectives  264 us (19%)
  other arithmetic  143 us (10%)
  local copies, waits for them, and re-layouts  140 us (10%)
  between operations  19 us (1%)
    psum x1, waiting for transfers between devices, local(): lax.psum(jnp.einsum('nf,df->nd', d_hidden, back_up, preferred_element_typ...  73.7 us
    reduce_scatter x1, waiting for transfers between devices, local(): lax.psum_scatter(grad_qkv, 'pages', scatter_dimension=0, tiled=True)  73.2 us
    reduce_scatter x1, waiting for transfers between devices, local(): lax.psum_scatter(grad_down, 'pages', scatter_dimension=0, tiled=True)  73.1 us
    reduce_scatter x1, waiting for transfers between devices, local(): lax.psum_scatter(grad_up, 'pages', scatter_dimension=0, tiled=True)  72.8 us
    reduce_scatter x1, waiting for transfers between devices, local(): lax.psum_scatter(grad_out, 'pages', scatter_dimension=0, tiled=True)  64 us
    psum x1, waiting for transfers between devices, local(): lax.psum(jnp.dot(activated, down_full, preferred_element_type=f32).astype...  62.7 us
    unnamed x18, waiting for transfers between devices  54 us
    dot_general x8, matrix products, page_scores(): jnp.einsum('chib,cjb->hij', left_part, placed, preferred_element_type=jnp...  48 us
  transfers between devices with their start and end apart: 14, of which 9 were waited for; matrix products, arithmetic and copies ran while one was open for 17% of the time, Pallas kernels for 0%

commit v1 on v0

v1 whole, which is shorter than its diff:
```python
import functools

import jax
import jax.numpy as jnp
from jax import lax
from jax.experimental import pallas as pl
from jax.experimental.pallas import tpu as pltpu
from jax.sharding import PartitionSpec as P

HD = 64
TXT = 512
GRID = 7
NB = 128


HIGHEST = lax.Precision.HIGHEST
EPSILON = 1e-05


def layer_norm(values, gain_row, shift_row):
    average = jnp.mean(values, -1, keepdims=True)
    centred = values - average
    variance = jnp.mean(centred * centred, -1, keepdims=True)
    return centred * lax.rsqrt(variance + EPSILON) * gain_row + shift_row


def valid_slots(text_len, seq_len):
    positions = jnp.arange(seq_len, dtype=jnp.int32)
    return jnp.logical_or(positions[None, :] < text_len[:, None], positions[None, :] >= TXT)


def offset_table():
    span_ids = jnp.arange(2 * NB, dtype=jnp.int32)
    offsets = span_ids[None, :] - span_ids[:, None]
    bucket_of = jnp.clip(offsets, -(NB // 2), NB // 2 - 1) + NB // 2
    return (bucket_of[:, :, None] == jnp.arange(NB, dtype=jnp.int32)[None, None, :]).astype(
        jnp.bfloat16
    )


def placed_of(coords_page):
    return (coords_page[:, :, None] == jnp.arange(2 * NB, dtype=jnp.int32)[None, None, :]).astype(
        jnp.bfloat16
    )


def toeplitz_of(offsets_map, rel_table):
    return jnp.einsum(
        "abk,ckh->chab", offsets_map, rel_table, preferred_element_type=jnp.float32
    ).astype(jnp.bfloat16)


def dcpe(field, valid, grid_index, kernel, first_bias, second_bias):
    page_count = field.shape[0]
    model_width = field.shape[-1]
    cell_count = GRID * GRID
    masked = field * valid[:, :, None].astype(field.dtype)
    text_part = masked[:, :TXT]
    padded = jnp.pad(text_part, ((0, 0), (3, 3), (0, 0)))
    text_out = jnp.zeros_like(text_part) + first_bias
    for spacing in range(1, 4):
        for offset_no in range(3):
            shift_at = 3 + (offset_no - 1) * spacing
            text_out = (
                text_out
                + kernel[3 * (spacing - 1) + offset_no] * padded[:, shift_at : shift_at + TXT]
            )
    placement = (
        grid_index[:, :, None] == jnp.arange(cell_count, dtype=jnp.int32)[None, None, :]
    ).astype(field.dtype)
    on_grid = jnp.einsum("psc,psd->pcd", placement, masked[:, TXT:], precision=HIGHEST)
    on_grid = jnp.pad(
        on_grid.reshape(page_count, GRID, GRID, model_width), ((0, 0), (1, 1), (1, 1), (0, 0))
    )
    grid_out = jnp.zeros((page_count, GRID, GRID, model_width), field.dtype) + second_bias
    for row_no in range(3):
        for col_no in range(3):
            grid_out = (
                grid_out
                + kernel[9 + 3 * row_no + col_no]
                * on_grid[:, row_no : row_no + GRID, col_no : col_no + GRID]
            )
    patch_out = jnp.einsum(
        "psc,pcd->psd",
        placement,
        grid_out.reshape(page_count, cell_count, model_width),
        precision=HIGHEST,
    )
    return jnp.concatenate([text_out, patch_out], 1)


def page_scores(queries, key_rows, valid_page, placed, toeplitz):
    products = (
        jnp.einsum("ihd,jhd->hij", queries, key_rows, preferred_element_type=jnp.float32) * 0.125
    )
    left_part = jnp.einsum(
        "cia,chab->chib", placed, toeplitz, preferred_element_type=jnp.float32
    ).astype(jnp.bfloat16)
    rel_terms = jnp.einsum("chib,cjb->hij", left_part, placed, preferred_element_type=jnp.float32)
    return jnp.where(valid_page[None, None, :], products + rel_terms, -1e30)


def attend_page(queries, key_rows, value_rows, valid_page, coords_page, toeplitz):
    scores = page_scores(queries, key_rows, valid_page, placed_of(coords_page), toeplitz)
    highest = jnp.max(scores, -1, keepdims=True)
    weights = jnp.exp(scores - highest)
    norm_total = jnp.sum(weights, -1, keepdims=True)
    probs = (weights / norm_total).astype(jnp.bfloat16)
    mixed = jnp.einsum(
        "hij,jhd->ihd", probs, value_rows, preferred_element_type=jnp.float32
    ).astype(jnp.bfloat16)
    return (mixed, (highest + jnp.log(norm_total))[..., 0])


def back_page(queries, key_rows, value_rows, valid_page, coords_page, toeplitz, log_total, d_mixed):
    placed = placed_of(coords_page)
    scores = page_scores(queries, key_rows, valid_page, placed, toeplitz)
    probs = jnp.exp(scores - log_total[..., None])
    d_probs = jnp.einsum("ihd,jhd->hij", d_mixed, value_rows, preferred_element_type=jnp.float32)
    centre = jnp.sum(probs * d_probs, -1, keepdims=True)
    d_scores = (probs * (d_probs - centre)).astype(jnp.bfloat16)
    d_query = (
        jnp.einsum("hij,jhd->ihd", d_scores, key_rows, preferred_element_type=jnp.float32) * 0.125
    ).astype(jnp.bfloat16)
    d_key = (
        jnp.einsum("hij,ihd->jhd", d_scores, queries, preferred_element_type=jnp.float32) * 0.125
    ).astype(jnp.bfloat16)
    d_value = jnp.einsum(
        "hij,ihd->jhd", probs.astype(jnp.bfloat16), d_mixed, preferred_element_type=jnp.float32
    ).astype(jnp.bfloat16)
    spread = jnp.einsum("cia,hij->chaj", placed, d_scores, preferred_element_type=jnp.float32)
    table_grad = jnp.einsum("chaj,cjb->chab", spread, placed.astype(jnp.float32), precision=HIGHEST)
    return (d_query, d_key, d_value, table_grad)


MESH = pl.DeviceIdType.MESH


def place():
    p, h = lax.axis_index("pages"), lax.axis_index("heads")
    return p, h, p // 2, p % 2, h // 2, h % 2


def greet(devices, count):
    barrier = pltpu.get_barrier_semaphore()
    for device in devices:
        pl.semaphore_signal(barrier, inc=1, device_id=device, device_id_type=MESH)
    pl.semaphore_wait(barrier, count)


def neighbours(p, h, z, y, x, c, n_z):
    core = (p, 2 * x + 1 - c)
    across = (p, 2 * (1 - x) + c)
    beside = (2 * z + 1 - y, h)
    line = [(2 * lax.rem(z + dz, n_z) + y, h) for dz in range(1, n_z)]
    return core, across, beside, line


def gather_kernel(n_p, late, early, *refs):
    n = len(late) + len(early)
    srcs, dsts = refs[:n], refs[n : 2 * n]
    send_sem, recv_sem, local_sem = refs[2 * n :]
    n_z = n_p // 2
    p, h, z, y, x, c = place()
    core, across, beside, line = neighbours(p, h, z, y, x, c, n_z)
    greet([core, across, beside] + line, 3 + len(line))
    h_x = 2 * (1 - x) + c

    n_line = n_z - 1
    started = []

    def copy(k, src, bh, bp, device, slot):
        return pltpu.make_async_remote_copy(
            src_ref=src,
            dst_ref=dsts[k].at[bh, bp],
            send_sem=send_sem.at[k, slot],
            recv_sem=recv_sem.at[k, bh, bp],
            device_id=device,
            device_id_type=MESH,
        )

    used = [0] * n

    def send(k, bh, bp, device, own=False):
        src = srcs[k] if own else dsts[k].at[bh, bp]
        item = copy(k, src, bh, bp, device, used[k])
        used[k] += 1
        item.start()
        started.append(item)

    def arrived(k, bh, bp):
        copy(k, dsts[k].at[bh, bp], bh, bp, core, 0).wait_recv()

    for k in early:
        send(k, h, p, across, own=True)
    for device in line:
        for k in late:
            send(k, h, p, device, own=True)
    for k in late:
        send(k, h, p, beside, own=True)
        send(k, h, p, across, own=True)
    for device in line:
        for k in early:
            send(k, h, p, device, own=True)
    for k in early:
        send(k, h, p, beside, own=True)
    for k in late + early:
        send(k, h, p, core, own=True)
    locals_ = []
    for k in range(n):
        item = pltpu.make_async_copy(srcs[k], dsts[k].at[h, p], local_sem.at[k])
        item.start()
        locals_.append(item)
    for k in early:
        arrived(k, h_x, p)
        for device in line:
            send(k, h_x, p, device)
        send(k, h_x, p, beside)
        send(k, h_x, p, core)
    for dz in range(1, n_z):
        q = 2 * lax.rem(z + n_z - dz, n_z) + y
        for k in late:
            arrived(k, h, q)
            send(k, h, q, beside)
            send(k, h, q, across)
            send(k, h, q, core)
        for k in early:
            for bh in (h, h_x):
                arrived(k, bh, q)
                send(k, bh, q, beside)
                send(k, bh, q, core)
    for dz in range(n_z):
        q = 2 * lax.rem(z + n_z - dz, n_z) + 1 - y
        for k in late:
            arrived(k, h, q)
            send(k, h, q, across)
            send(k, h, q, core)
        for k in early:
            for bh in (h, h_x):
                arrived(k, bh, q)
                send(k, bh, q, core)
    for k in late:
        for dz in range(n_z):
            for side in (y, 1 - y):
                q = 2 * lax.rem(z + n_z - dz, n_z) + side
                arrived(k, h_x, q)
                send(k, h_x, q, core)
    for k in late + early:
        for bx in (x, 1 - x):
            for dz in range(n_z):
                for side in (y, 1 - y):
                    q = 2 * lax.rem(z + n_z - dz, n_z) + side
                    arrived(k, 2 * bx + 1 - c, q)
    for item in locals_:
        item.wait()
    for item in started:
        item.wait_send()


def gather_all(shards, n_h, n_p, late, early):
    outs = [jax.ShapeDtypeStruct((n_h, n_p) + s.shape, s.dtype) for s in shards]
    n = len(shards)
    total = n_h * n_p
    if n_h != 4 or total > 32:
        return [
            lax.all_gather(lax.all_gather(s, "pages", axis=0), "heads", axis=0) for s in shards
        ]
    return pl.pallas_call(
        functools.partial(gather_kernel, n_p, late, early),
        name="gather_weights",
        out_shape=outs,
        in_specs=[pl.BlockSpec(memory_space=pltpu.VMEM)] * n,
        out_specs=[pl.BlockSpec(memory_space=pl.ANY)] * n,
        scratch_shapes=[
            pltpu.SemaphoreType.DMA((n, total)),
            pltpu.SemaphoreType.DMA((n, n_h, n_p)),
            pltpu.SemaphoreType.DMA((n,)),
        ],
        compiler_params=pltpu.CompilerParams(collective_id=0, has_side_effects=True),
    )(*shards)


def reduce_kernel(n_p, late, early, *refs):
    n = len(late) + len(early)
    srcs, dsts = refs[:n], refs[n : 2 * n]
    boxes = refs[2 * n : 6 * n]
    r1, r2, r3, r4 = boxes[:n], boxes[n : 2 * n], boxes[2 * n : 3 * n], boxes[3 * n :]
    send_sem, recv_sem = refs[6 * n :]
    n_z = n_p // 2
    p, h, z, y, x, c = place()
    core, across, beside, line = neighbours(p, h, z, y, x, c, n_z)
    greet([core, across, beside] + line, 3 + len(line))
    f32 = jnp.float32
    at2, at3, at4 = 2 * n_p, 4 * n_p, 6 * n_p

    def copy(k, src, dst, slot, device, out_slot=None):
        return pltpu.make_async_remote_copy(
            src_ref=src,
            dst_ref=dst,
            send_sem=send_sem.at[k, slot if out_slot is None else out_slot],
            recv_sem=recv_sem.at[k, slot],
            device_id=device,
            device_id_type=MESH,
        )

    def page_of(i):
        return 2 * lax.rem(z + lax.div(i, 2) + 1, n_z) + lax.rem(1 - y + i, 2)

    def core_copy(k, xh, q):
        return copy(k, srcs[k].at[2 * xh + 1 - c, q], r1[k].at[xh, q], xh * n_p + q, core)

    def x_copy(k, q):
        return copy(k, r1[k].at[1 - x, q], r2[k].at[q], at2 + q, across)

    def y_copy(k, zq):
        return copy(k, r1[k].at[x, 2 * zq + 1 - y], r3[k].at[zq], at3 + zq, beside)

    def z_copy(k, zq, device):
        return copy(k, r1[k].at[x, 2 * zq + y], r4[k].at[z], at4 + z, device, at4 + zq)

    def z_wait(k, zq):
        return copy(k, r4[k].at[zq], r4[k].at[zq], at4 + zq, core)

    def y2_copy(k, xh, zq):
        return copy(k, r1[k].at[xh, 2 * zq + 1 - y], r2[k].at[xh, zq], at2 + xh * n_z + zq, beside)

    def z2_copy(k, xh, zq, device):
        src = r1[k].at[xh, 2 * zq + y]
        return copy(k, src, r3[k].at[xh, z], at3 + xh * n_z + z, device, at3 + xh * n_z + zq)

    def z2_wait(k, xh, zq):
        return copy(k, r3[k].at[xh, zq], r3[k].at[xh, zq], at3 + xh * n_z + zq, core)

    def x2_copy(k):
        return copy(k, r1[k].at[1 - x, 2 * z + y], r4[k].at[0], at4, across)

    def each(count, body):
        lax.fori_loop(0, count, lambda i, carry: (body(i), carry)[1], jnp.int32(0))

    def begin_late(i):
        for k in late:
            core_copy(k, 1 - x, page_of(i)).start()

    def begin_early(i):
        for xh in (1 - x, x):
            for k in early:
                core_copy(k, xh, 2 * lax.rem(z + i + 1, n_z) + y).start()

    def begin_early_y(i):
        for xh in (1 - x, x):
            for k in early:
                core_copy(k, xh, 2 * lax.rem(z + i + 1, n_z) + 1 - y).start()

    def begin_rest(i):
        for k in late:
            core_copy(k, x, page_of(i)).start()

    each(n_p, begin_late)
    each(n_z, begin_early_y)
    each(n_p, begin_rest)
    each(n_z, begin_early)

    def x_stage(i):
        q = page_of(i)
        for k in late:
            core_copy(k, 1 - x, q).wait_recv()
            total = srcs[k][2 * (1 - x) + c, q].astype(f32) + r1[k][1 - x, q].astype(f32)
            r1[k][1 - x, q] = total.astype(r1[k].dtype)
        for k in late:
            x_copy(k, q).start()

    def early_y_stage(i):
        zq = lax.rem(z + i + 1, n_z)
        q = 2 * zq + 1 - y
        for k in early:
            for xh in (1 - x, x):
                core_copy(k, xh, q).wait_recv()
                total = srcs[k][2 * xh + c, q].astype(f32) + r1[k][xh, q].astype(f32)
                r1[k][xh, q] = total.astype(r1[k].dtype)
        for k in early:
            for xh in (1 - x, x):
                y2_copy(k, xh, zq).start()

    def both(i):
        x_stage(2 * i)
        x_stage(2 * i + 1)
        early_y_stage(i)

    each(n_z, both)

    def early_z_stage(i):
        zq = lax.rem(z + i + 1, n_z)
        q = 2 * zq + y
        for k in early:
            for xh in (1 - x, x):
                core_copy(k, xh, q).wait_recv()
                y2_copy(k, xh, zq).wait_recv()
                total = srcs[k][2 * xh + c, q].astype(f32) + r1[k][xh, q].astype(f32)
                total = total + r2[k][xh, zq].astype(f32)
                r1[k][xh, q] = total.astype(r1[k].dtype)
        return zq

    def late_y_stage(i):
        zq = lax.rem(z + i + 1, n_z)
        q = 2 * zq + 1 - y
        for k in late:
            core_copy(k, x, q).wait_recv()
            x_copy(k, q).wait_recv()
            total = srcs[k][h, q].astype(f32) + r1[k][x, q].astype(f32) + r2[k][q].astype(f32)
            r1[k][x, q] = total.astype(r1[k].dtype)
        for k in late:
            y_copy(k, zq).start()

    def late_z_stage(i):
        zq = lax.rem(z + i + 1, n_z)
        q = 2 * zq + y
        for k in late:
            core_copy(k, x, q).wait_recv()
            x_copy(k, q).wait_recv()
            y_copy(k, zq).wait_recv()
            total = srcs[k][h, q].astype(f32) + r1[k][x, q].astype(f32)
            total = total + r2[k][q].astype(f32) + r3[k][zq].astype(f32)
            r1[k][x, q] = total.astype(r1[k].dtype)
        return zq

    def early_line(i):
        zq = early_z_stage(i)
        for k in early:
            for xh in (1 - x, x):
                z2_copy(k, xh, zq, (2 * zq + y, h)).start()

    def late_line(i):
        zq = late_z_stage(i)
        for k in late:
            z_copy(k, zq, (2 * zq + y, h)).start()

    def stage_two(i):
        late_y_stage(i)

    each(n_z, stage_two)
    each(n_z - 1, early_line)
    each(n_z - 1, late_line)

    mine = 2 * z + y
    for k in early:
        for xh in (1 - x, x):
            core_copy(k, xh, mine).wait_recv()
            y2_copy(k, xh, z).wait_recv()
        total = srcs[k][2 * (1 - x) + c, mine].astype(f32) + r1[k][1 - x, mine].astype(f32)
        total = total + r2[k][1 - x, z].astype(f32)
        for dz in range(1, n_z):
            zq = lax.rem(z + n_z - dz, n_z)
            z2_wait(k, 1 - x, zq).wait_recv()
            total = total + r3[k][1 - x, zq].astype(f32)
        r1[k][1 - x, mine] = total.astype(r1[k].dtype)
        x2_copy(k).start()
    for k in late:
        core_copy(k, x, mine).wait_recv()
        x_copy(k, mine).wait_recv()
        y_copy(k, z).wait_recv()
        total = srcs[k][h, mine].astype(f32) + r1[k][x, mine].astype(f32)
        total = total + r2[k][mine].astype(f32) + r3[k][z].astype(f32)
        for dz in range(1, n_z):
            zq = lax.rem(z + n_z - dz, n_z)
            z_wait(k, zq).wait_recv()
            total = total + r4[k][zq].astype(f32)
        dsts[k][...] = total
    for k in early:
        total = srcs[k][h, mine].astype(f32) + r1[k][x, mine].astype(f32) + r2[k][x, z].astype(f32)
        for dz in range(1, n_z):
            zq = lax.rem(z + n_z - dz, n_z)
            z2_wait(k, x, zq).wait_recv()
            total = total + r3[k][x, zq].astype(f32)
        x2_copy(k).wait_recv()
        dsts[k][...] = total + r4[k][0].astype(f32)

    def sent_pages(q):
        for k in range(n):
            for xh in (0, 1):
                core_copy(k, xh, q).wait_send()
        for k in late:
            x_copy(k, q).wait_send()

    def sent_lines(zq):
        for k in late:
            y_copy(k, zq).wait_send()
        for k in early:
            for xh in (0, 1):
                y2_copy(k, xh, zq).wait_send()

    each(n_p, sent_pages)
    each(n_z, sent_lines)
    for k in early:
        x2_copy(k).wait_send()

    def sent_peer(i):
        zq = lax.rem(z + i + 1, n_z)
        for k in late:
            z_copy(k, zq, core).wait_send()
        for k in early:
            for xh in (0, 1):
                z2_copy(k, xh, zq, core).wait_send()

    each(n_z - 1, sent_peer)


def reduce_all(grads, n_h, n_p, late, early):
    outs = [jax.ShapeDtypeStruct(g.shape[2:], jnp.float32) for g in grads]
    n = len(grads)
    n_z = n_p // 2
    if n_h != 4 or n_h * n_p > 32:
        parts = [lax.psum_scatter(g.astype(jnp.float32), "heads", scatter_dimension=0) for g in grads]
        return [lax.psum_scatter(g, "pages", scatter_dimension=0) for g in parts]
    boxes = [[], [], [], []]
    for k, g in enumerate(grads):
        tail = g.shape[2:]
        leads = [(2, n_p), (n_p,), (n_z,), (n_z,)]
        if k in early:
            leads = [(2, n_p), (2, n_z), (2, n_z), (1,)]
        for box, lead in zip(boxes, leads):
            box.append(pltpu.VMEM(lead + tail, g.dtype))
    return pl.pallas_call(
        functools.partial(reduce_kernel, n_p, late, early),
        name="reduce_grads",
        out_shape=outs,
        in_specs=[pl.BlockSpec(memory_space=pltpu.VMEM)] * n,
        out_specs=[pl.BlockSpec(memory_space=pltpu.VMEM)] * n,
        scratch_shapes=sum(boxes, [])
        + [
            pltpu.SemaphoreType.DMA((n, 7 * n_p)),
            pltpu.SemaphoreType.DMA((n, 7 * n_p)),
        ],
        compiler_params=pltpu.CompilerParams(collective_id=1, has_side_effects=True),
    )(*grads)


def share_kernel(n, *refs):
    srcs, dsts = refs[:n], refs[n : 2 * n]
    send_sem, recv_sem, local_sem = refs[2 * n :]
    p, h = lax.axis_index("pages"), lax.axis_index("heads")
    x, c = h // 2, h % 2
    core, across = (p, 2 * x + 1 - c), (p, 2 * (1 - x) + c)
    greet([core, across], 2)
    h_x = 2 * (1 - x) + c

    def copy(k, src, bh, device, slot):
        return pltpu.make_async_remote_copy(
            src_ref=src,
            dst_ref=dsts[k].at[bh],
            send_sem=send_sem.at[k, slot],
            recv_sem=recv_sem.at[k, bh],
            device_id=device,
            device_id_type=MESH,
        )

    started = []
    for k in range(n):
        item = copy(k, srcs[k], h, across, 0)
        item.start()
        started.append(item)
    for k in range(n):
        item = copy(k, srcs[k], h, core, 1)
        item.start()
        started.append(item)
    own = []
    for k in range(n):
        item = pltpu.make_async_copy(srcs[k], dsts[k].at[h], local_sem.at[k])
        item.start()
        own.append(item)
    for k in range(n):
        copy(k, dsts[k].at[h_x], h_x, core, 0).wait_recv()
        item = copy(k, dsts[k].at[h_x], h_x, core, 2)
        item.start()
        started.append(item)
    for k in range(n):
        for bx in (x, 1 - x):
            bh = 2 * bx + 1 - c
            copy(k, dsts[k].at[bh], bh, core, 0).wait_recv()
    for item in own:
        item.wait()
    for item in started:
        item.wait_send()


def share_pages(pages, n_h):
    n = len(pages)
    if n_h != 4:
        return [lax.all_gather(page, "heads", axis=0) for page in pages]
    return pl.pallas_call(
        functools.partial(share_kernel, n),
        name="share_pages",
        out_shape=[jax.ShapeDtypeStruct((n_h,) + page.shape, page.dtype) for page in pages],
        in_specs=[pl.BlockSpec(memory_space=pltpu.VMEM)] * n,
        out_specs=[pl.BlockSpec(memory_space=pl.ANY)] * n,
        scratch_shapes=[
            pltpu.SemaphoreType.DMA((n, 3)),
            pltpu.SemaphoreType.DMA((n, n_h)),
            pltpu.SemaphoreType.DMA((n,)),
        ],
        compiler_params=pltpu.CompilerParams(collective_id=2, has_side_effects=True),
    )(*pages)


def pack_small(conv_w, biases, gains, b_qv, b_up, rel_bias):
    flat = jnp.concatenate(
        [v.reshape(-1) for v in (conv_w, biases, gains, b_qv, b_up, rel_bias)]
    )
    room = -flat.shape[0] % 1024
    return jnp.pad(flat, (0, room)).reshape(-1, 128)


def unpack_small(blocks, sizes):
    n_h, n_p = blocks.shape[:2]
    flat = blocks.reshape(n_h, n_p, -1)
    parts, at = [], 0
    for shape in sizes:
        count = 1
        for extent in shape:
            count *= extent
        parts.append(flat[:, :, at : at + count].reshape((n_h, n_p) + shape))
        at += count
    return parts


def local(
    x_in,
    cotangent,
    text_len,
    coords,
    grid_index,
    w_qkv,
    b_qv,
    w_out,
    w_up,
    b_up,
    w_down,
    rel_bias,
    conv_w,
    biases,
    gains,
    n_h,
    n_p,
):
    f32 = jnp.float32
    bf16 = jnp.bfloat16
    head_id = lax.axis_index("heads")
    seq_len, model_width = x_in.shape[1:]
    part = w_qkv.shape[2]
    heads_here = part // HD
    n_heads = heads_here * n_h
    rows_in = w_qkv.shape[0]
    small_sizes = [v.shape for v in (conv_w, biases, gains, b_qv, b_up, rel_bias)]
    late, early = [0, 1, 2, 3], [4]
    gathered = gather_all(
        [
            pack_small(conv_w, biases, gains, b_qv, b_up, rel_bias),
            w_qkv.reshape(rows_in, 3 * part),
            w_out,
            w_up,
            w_down,
        ],
        n_h,
        n_p,
        late,
        early,
    )
    conv_s, bias_s, gain_s, bqv_s, bup_s, rel_s = unpack_small(gathered[0], small_sizes)

    def columns(blocks):
        return jnp.transpose(blocks, (2, 1, 0, 3)).reshape(blocks.shape[2], -1)

    kernel_float = columns(conv_s).astype(f32)
    bias_float = columns(bias_s).astype(f32)
    gain_float = columns(gain_s).astype(f32)
    bqv_full = jnp.transpose(bqv_s, (2, 0, 1, 3)).reshape(2, n_h, part).astype(f32)
    bup_full = bup_s.reshape(-1).astype(f32)
    rel_full = jnp.transpose(rel_s, (2, 1, 3, 0, 4)).reshape(3, NB, n_heads)
    qkv_full = gathered[1].reshape(n_h, model_width, 3 * part)
    out_full = gathered[2].reshape(n_h, part, model_width)
    up_full = gathered[3].reshape(n_h, model_width, -1)
    down_full = gathered[4].reshape(n_h, up_full.shape[2], model_width)

    def mine(values):
        return lax.dynamic_index_in_dim(values, head_id, 0, keepdims=True)

    x_page, cot_page = mine(x_in), mine(cotangent)
    len_page, coords_page, grid_page = mine(text_len), mine(coords)[0], mine(grid_index)
    offsets_map = offset_table()
    toeplitz = toeplitz_of(offsets_map, rel_full)
    valid = valid_slots(len_page, seq_len)

    def conv_part(values, kernel, first_bias, second_bias):
        return dcpe(values, valid, grid_page, kernel, first_bias, second_bias)

    field = x_page.astype(f32)
    h_one = (field + conv_part(field, kernel_float, bias_float[0], bias_float[1]))[0]
    act_in = h_one.astype(bf16)
    qkv_bias = jnp.concatenate([bqv_full[0], jnp.zeros_like(bqv_full[0]), bqv_full[1]], -1)
    projected = (
        jnp.einsum("nd,hde->hne", act_in, qkv_full, preferred_element_type=f32)
        + qkv_bias[:, None, :]
    ).astype(bf16)

    def split(values):
        values = values.reshape(n_h, seq_len, heads_here, HD)
        return jnp.transpose(values, (1, 0, 2, 3)).reshape(seq_len, n_heads, HD)

    queries = split(projected[:, :, :part])
    key_rows = split(projected[:, :, part : 2 * part])
    value_rows = split(projected[:, :, 2 * part :])
    heads_out, log_total = attend_page(
        queries, key_rows, value_rows, valid[0], coords_page, toeplitz
    )
    mixed = heads_out.reshape(seq_len, n_h, part)
    attn = (
        jnp.sum(
            jnp.einsum("nhc,hcd->hnd", mixed, out_full, preferred_element_type=f32)
            .astype(bf16)
            .astype(f32),
            0,
        )
        + bias_float[2]
    )
    h_two_pre = h_one + attn
    h_two = layer_norm(h_two_pre, gain_float[0], bias_float[3])
    ffn_in = h_two.astype(bf16)
    bup_groups = bup_full.reshape(n_h, 1, -1)
    hidden = jnp.einsum("nd,hdf->hnf", ffn_in, up_full, preferred_element_type=f32) + bup_groups
    activated = jax.nn.gelu(hidden, approximate=False).astype(bf16)
    ffn = (
        jnp.sum(
            jnp.einsum("hnf,hfd->hnd", activated, down_full, preferred_element_type=f32)
            .astype(bf16)
            .astype(f32),
            0,
        )
        + bias_float[4]
    )
    summed = h_two + ffn
    result = layer_norm(summed, gain_float[1], bias_float[5])

    d_result = cot_page[0].astype(f32)
    norm_two_back = jax.vjp(layer_norm, summed, gain_float[1], bias_float[5])[1]
    d_sum, d_gain_two, d_shift_two = norm_two_back(d_result)
    d_ffn = d_sum.astype(bf16)
    grad_bias_down = jnp.sum(d_ffn.astype(f32), 0)
    grad_down = jnp.einsum("hnf,nd->hfd", activated, d_ffn, preferred_element_type=f32)
    d_act = jnp.einsum("nd,hfd->hnf", d_ffn, down_full, preferred_element_type=f32)
    gelu_back = jax.vjp(lambda inner: jax.nn.gelu(inner, approximate=False), hidden)[1]
    d_hidden = gelu_back(d_act)[0].astype(bf16)
    grad_up_bias = jnp.sum(d_hidden.astype(f32), 1)
    grad_up = jnp.einsum("nd,hnf->hdf", ffn_in, d_hidden, preferred_element_type=f32)
    d_two = d_sum + jnp.einsum("hnf,hdf->nd", d_hidden, up_full, preferred_element_type=f32)
    norm_one_back = jax.vjp(layer_norm, h_two_pre, gain_float[0], bias_float[3])[1]
    d_pre, d_gain_one, d_shift_one = norm_one_back(d_two)
    d_attn = d_pre.astype(bf16)
    grad_out_bias = jnp.sum(d_attn.astype(f32), 0)
    grad_out = jnp.einsum("nhc,nd->hcd", mixed, d_attn, preferred_element_type=f32)
    d_mixed = jnp.einsum("nd,hcd->nhc", d_attn, out_full, preferred_element_type=f32).astype(bf16)
    d_query, d_key, d_value, table_grad = back_page(
        queries,
        key_rows,
        value_rows,
        valid[0],
        coords_page,
        toeplitz,
        log_total,
        d_mixed.reshape(seq_len, n_heads, HD),
    )
    grad_rel = jnp.einsum("abk,chab->ckh", offsets_map.astype(f32), table_grad, precision=HIGHEST)

    def join(values):
        return jnp.transpose(values.reshape(seq_len, n_h, part), (1, 0, 2))

    d_proj = jnp.concatenate([join(d_query), join(d_key), join(d_value)], -1)
    grad_qkv = jnp.einsum("nd,hne->hde", act_in, d_proj, preferred_element_type=f32)
    row_sums = jnp.sum(d_proj.astype(f32), 1)
    grad_qv_bias = jnp.stack([row_sums[:, :part], row_sums[:, 2 * part :]])
    d_one = d_pre + jnp.einsum("hne,hde->nd", d_proj, qkv_full, preferred_element_type=f32)
    conv_back = jax.vjp(conv_part, field, kernel_float, bias_float[0], bias_float[1])[1]
    d_field, grad_kernel, d_first, d_second = conv_back(d_one[None])
    grad_x = d_one + d_field[0]
    grad_bias_rows = jnp.stack(
        [d_first, d_second, grad_out_bias, d_shift_one, grad_bias_down, d_shift_two]
    )
    grad_gain_rows = jnp.stack([d_gain_one, d_gain_two])

    def uncolumns(values):
        rows = values.shape[0]
        return jnp.transpose(values.reshape(rows, n_p, n_h, -1), (2, 1, 0, 3)).reshape(n_h, n_p, -1)

    flat = jnp.concatenate(
        [
            uncolumns(grad_kernel),
            uncolumns(grad_bias_rows),
            uncolumns(grad_gain_rows),
            jnp.transpose(grad_qv_bias.reshape(2, n_h, n_p, -1), (1, 2, 0, 3)).reshape(n_h, n_p, -1),
            grad_up_bias.reshape(n_h, n_p, -1),
            jnp.transpose(
                grad_rel.reshape(3, n_p, -1, n_h, heads_here), (3, 1, 0, 2, 4)
            ).reshape(n_h, n_p, -1),
        ],
        -1,
    )
    width = flat.shape[2]
    flat = jnp.pad(flat, ((0, 0), (0, 0), (0, -width % 1024))).reshape(n_h, n_p, -1, 128)

    def blocks(values):
        return values.reshape((n_h, n_p, -1) + values.shape[2:]).astype(bf16)

    reduced = reduce_all(
        [flat, blocks(grad_qkv), blocks(grad_out), blocks(grad_up), blocks(grad_down)],
        n_h,
        n_p,
        late,
        early,
    )
    small = unpack_small(reduced[0][None, None], small_sizes)
    small = [value[0, 0] for value in small]
    out_all, grad_x_all = share_pages([result.astype(bf16), grad_x.astype(bf16)], n_h)
    return (
        out_all,
        grad_x_all.astype(f32),
        reduced[1].reshape(rows_in, 3, part),
        small[3],
        reduced[2],
        reduced[3],
        small[4],
        reduced[4],
        small[5],
        small[0],
        small[1],
        small[2],
    )


def solution(mesh):
    n_h, n_p = mesh.shape["heads"], mesh.shape["pages"]
    return jax.shard_map(
        functools.partial(local, n_h=n_h, n_p=n_p),
        mesh=mesh,
        in_specs=(
            P("pages", None, None),
            P("pages", None, None),
            P("pages"),
            P("pages", None, None),
            P("pages", None),
            P("pages", None, "heads"),
            P(None, ("heads", "pages")),
            P(("heads", "pages"), None),
            P("pages", "heads"),
            P(("heads", "pages")),
            P(("heads", "pages"), None),
            P(None, "pages", "heads"),
            P(None, ("pages", "heads")),
            P(None, ("pages", "heads")),
            P(None, ("pages", "heads")),
        ),
        out_specs=(
            P("pages", None, None),
            P("pages", None, None),
            P("pages", None, "heads"),
            P(None, ("heads", "pages")),
            P(("heads", "pages"), None),
            P("pages", "heads"),
            P(("heads", "pages")),
            P(("heads", "pages"), None),
            P(None, "pages", "heads"),
            P(None, ("pages", "heads")),
            P(None, ("pages", "heads")),
            P(None, ("pages", "heads")),
        ),
        check_vma=False,
    )
```

time: 1400 us -> 736 us (0.53)
  waiting for transfers between devices: 520 us -> 0 us
  blocking collectives: 264 us -> 0 us
  Pallas kernels: 0 us -> 261 us
  matrix products: 297 us -> 239 us
  other arithmetic: 143 us -> 86.7 us
  between operations: 19 us -> 2.74 us
    reduce_scatter x4 -> x0, waiting for transfers between devices: 283 us -> none  [the longest x1 73.2 us: local(): lax.psum_scatter(grad_qkv, 'pages', scatter_dimension=0, tiled=True)]
    pallas_call x0 -> x3, Pallas kernels: none -> 261 us  [the longest x1 127 us: reduce_all(): pl.pallas_call(functools.partial(reduce_kernel, n_p, late, early), name='...]
    all_gather x7 -> x0, blocking collectives: 233 us -> none  [the longest x1 47.2 us: local(): lax.all_gather(gains, ('pages', 'heads'), axis=1, tiled=True)]
    psum x4 -> x0, waiting for transfers between devices: 182 us -> none  [the longest x1 73.7 us: local(): lax.psum(jnp.einsum('nf,df->nd', d_hidden, back_up, preferred_element_typ...]
    unnamed x18 -> x0, waiting for transfers between devices: 54 us -> none
    unnamed x2 -> x0, blocking collectives: 31.4 us -> none
    dot_general x8 -> x1, matrix products: 48 us -> 19.6 us  [page_scores(): jnp.einsum('chib,cjb->hij', left_part, placed, preferred_element_type=jnp...]
    reduce_sum x1, other arithmetic: 29.3 us -> 7.7 us  [dcpe(): kernel[3 * (spacing - 1) + offset_no] * padded[:, shift_at:shift_at + TXT]]
  transfers between devices with their start and end apart: 14 -> 0, of which waited for: 9 -> 0; matrix products, arithmetic and copies ran while one was open for 17% -> 0% of each run, Pallas kernels for 0% -> 0%
where the time goes in v1:
time: 736 us; the launch traced here: 724 us
  Pallas kernels  261 us (35%)
  matrix products  239 us (32%)
  local copies, waits for them, and re-layouts  135 us (18%)
  other arithmetic  86.7 us (12%)
    pallas_call x1, Pallas kernels, reduce_all(): pl.pallas_call(functools.partial(reduce_kernel, n_p, late, early), name='...  127 us
    pallas_call x1, Pallas kernels, gather_all(): pl.pallas_call(functools.partial(gather_kernel, n_p, late, early), name='...  89.9 us
    pallas_call x1, Pallas kernels, share_pages(): pl.pallas_call(functools.partial(share_kernel, n), name='share_pages', ou...  44.4 us
    dot_general x1, matrix products, local(): jnp.einsum('abk,chab->ckh', offsets_map.astype(f32), table_grad, precisio...  32.4 us
    unnamed x207, local copies, waits for them, and re-layouts  28.1 us
    dot_general x1, matrix products, back_page(): jnp.einsum('chaj,cjb->chab', spread, placed.astype(jnp.float32), precisio...  22.6 us
    dot_general x1, matrix products, local(): jnp.einsum('nd,hdf->hnf', ffn_in, up_full, preferred_element_type=f32)  21.5 us
    dot_general x1, matrix products, page_scores(): jnp.einsum('chib,cjb->hij', left_part, placed, preferred_element_type=jnp...  19.6 us

profile of v1, /device:TPU:9, one launch (start us, length us, event | category | flops | bytes accessed | tf_op | source)
XLA Modules:
  0.0 724.1 jit_solution(7309427553487048076)
XLA Ops:
  12.4 6.6 constant_dynamic-slice_fusion
  25.3 89.9 %gather_weights.1 = (bf16[4,8,8,128]{3,2,1,0:T(8,128)(2,1)}, bf16[4,8,96,576]{3,2,1,0:T(8,128)(2,1)}, bf16[4,8,24,768]{3,2,1,0:T(8,128)(2,1)}, bf16[4,8,96,768]{3,2,1,0:T(8,128)(2,1)}, bf16[4,8,96,768]{3,2,1,0:T(8,128)(2,1)}) custom-call(bf16[8,128]{1,0:T(8,128)(2,1)} %pad_bitcast_fusion.1.refs_0_, bf16[96,576]{1,0:T(8,128)(2,1)} %copy.123.refs_1_, ...), custom_call_target="tpu_custom_call" | custom-call | tf_op jit(solution)/shard_map/gather_weights/pallas_call | solution.py:268
  164.7 7.0 multiply_add_fusion.1
  184.0 17.3 %fusion.64 = bf16[3,12,256,256]{3,1,2,0:T(8,128)(2,1)} fusion(s32[256,256]{1,0:T(8,128)S(1)} %copy-done.32, bf16[3,128,12,1]{1,2,0,3:T(8,128)(2,1)S(1)} %copy-done.78), kind=kOutput, calls=%fused_computation.87 | convolution fusion | flops 614727680 | bytes 4989952 | tf_op jit(solution)/shard_map/abk,ckh->chab/dot_general | solution.py:48
  201.3 19.6 %fusion.13 = f32[12,561,561,1]{1,2,3,0:T(8,128)} fusion(bf16[3,12,256,256]{3,1,2,0:T(8,128)(2,1)} %fusion.64, s32[3,561]{1,0:T(4,128)S(1)} %bitcast.415), kind=kOutput, calls=%fused_computation.18 | convolution fusion | flops 8454099456 | bytes 19831932 | tf_op jit(solution)/shard_map/chib,cjb->hij/dot_general | solution.py:99
  221.0 16.3 %fusion.155 = (f32[12,561]{1,0:T(8,128)S(1)}, f32[12,561,561]{1,2,0:T(8,128)}) fusion(f32[12,561,561,1]{1,2,3,0:T(8,128)} %fusion.13, bf16[561,12,64]{0,2,1:T(8,128)(2,1)} %bitcast.385, bf16[561,12,64]{0,2,1:T(8,128)(2,1)S(1)} %bitcast.383, pred[561]{0:T(1024)(128)(4,1)S(1)} %copy-done.82), kind=kOutput, calls=%fused_computation.302 | convolution fusion | flops 498511296 | bytes 31964096 | tf_op jit(solution)/shard_map/ihd,jhd->hij/dot_general | solution.py:94
  237.3 8.5 %fusion.10 = f32[12,561]{1,0:T(8,128)S(1)} fusion(f32[12,561,561]{1,2,0:T(8,128)} %get-tuple-element.166, f32[12,561]{1,0:T(8,128)S(1)} %get-tuple-element.165), kind=kLoop, calls=%fused_computation.15 | loop fusion | flops 7546572 | bytes 15160464 | tf_op jit(solution)/shard_map/reduce_sum | solution.py:107
  246.4 9.3 %fusion.94 = bf16[12,64,561]{2,1,0:T(8,128)(2,1)S(1)} fusion(bf16[561,12,64]{0,2,1:T(8,128)(2,1)S(1)} %bitcast.401, f32[12,561,561]{1,2,0:T(8,128)} %get-tuple-element.166, f32[12,561]{1,0:T(8,128)S(1)} %fusion.10, f32[12,561]{1,0:T(8,128)S(1)} %get-tuple-element.165), kind=kOutput, calls=%fused_computation.162 | convolution fusion | flops 495172256 | bytes 16883856 | tf_op jit(solution)/shard_map/hij,jhd->ihd/dot_general | solution.py:109
  258.0 21.5 %fusion.25 = (f32[4,561,768]{2,1,0:T(8,128)}, f32[4,768,561]{1,2,0:T(8,128)}) fusion(f32[4,768]{1,0:T(4,128)S(1)} %reshape.1050, bf16[4,768,768]{2,1,0:T(8,128)(2,1)} %bitcast.425, f32[768]{0:T(1024)S(1)} %copy-done.67, f32[768]{0:T(1024)S(1)} %mul.710, f32[561]{0:T(1024)S(1)} %fusion.139, f32[561]{0:T(1024)S(1)} %broadcast_multiply_fusion.19, ...), kind=kOutput, calls=%fused_computation.29 | convolution fusion | flops 2758719744 | bytes 21978504 | tf_op jit(solution)/shard_map/nd,hdf->hnf/dot_general | solution.py:728
  279.5 9.4 %convert_reduce_fusion.1 = f32[561,768]{1,0:T(8,128)S(1)} fusion(bf16[4,768,768]{2,1,0:T(8,128)(2,1)} %bitcast.389, f32[4,561,768]{2,1,0:T(8,128)} %get-tuple-element.167, f32[4,768,561]{1,2,0:T(8,128)} %get-tuple-element.168, f32[4,768]{1,0:T(4,128)S(1)} %reshape.1050), kind=kOutput, calls=%fused_computation.62 | convolution fusion | flops 2658763008 | bytes 20241408 | tf_op jit(solution)/shard_map/hnf,hfd->hnd/dot_general | solution.py:732
  299.3 11.0 %convert_reduce_fusion = (f32[4,768]{1,0:T(4,128)}, bf16[4,561,768]{2,1,0:T(8,128)(2,1)S(1)}) fusion(f32[4,561,768]{2,1,0:T(8,128)} %get-tuple-element.167, bf16[4,768,768]{2,1,0:T(8,128)(2,1)} %bitcast.390, bf16[1,561,768]{2,1,0:T(8,128)(2,1)S(1)} %fusion.78, f32[4,768,561]{1,2,0:T(8,128)} %get-tuple-element.168, f32[4,768]{1,0:T(4,128)S(1)} %reshape.1050), kind=kOutput, calls=%fused_computation.61 | convolution fusion | flops 2676424704 | bytes 22838784 | tf_op jit(solution)/shard_map/nd,hfd->hnf/dot_general | solution.py:748
  310.3 16.3 %fusion.28 = bf16[4,768,561]{1,2,0:T(8,128)(2,1)} fusion(f32[4,768,561]{1,2,0:T(8,128)S(1)} %bitcast.378, f32[4,768]{1,0:T(4,128)S(1)} %reshape.1050), kind=kLoop, calls=%fused_computation.32 | loop fusion | flops 113743872 | bytes 10352640 | tf_op jit(solution)/shard_map/convert_element_type | solution.py:729
  347.2 8.0 %convolution_convert_fusion.1.refs_4_ = bf16[4,8,96,768]{3,2,1,0:T(8,128)(2,1)} fusion(bf16[4,8,96,561]{3,2,1,0:T(8,128)(2,1)} %bitcast.400, bf16[1,561,768]{2,1,0:T(8,128)(2,1)S(1)} %copy-done.29), kind=kOutput, calls=%fused_computation.91 | convolution fusion | flops 2649489408 | bytes 9027072 | tf_op jit(solution)/shard_map/hnf,nd->hfd/dot_general | solution.py:747
  359.4 8.8 %fusion.95 = bf16[12,64,561]{2,1,0:T(8,128)(2,1)S(1)} fusion(bf16[561,12,64]{0,2,1:T(8,128)(2,1)S(1)} %bitcast.403, f32[12,561,561]{1,2,0:T(8,128)} %get-tuple-element.166, f32[12,561]{1,0:T(8,128)S(1)} %copy-done.31), kind=kOutput, calls=%fused_computation.163 | convolution fusion | flops 491395616 | bytes 16856928 | tf_op jit(solution)/shard_map/hij,ihd->jhd/dot_general | solution.py:128
  369.6 11.1 %multiply_reduce_fusion = (f32[12,561]{1,0:T(8,128)S(1)}, f32[12,561,561]{1,2,0:T(8,128)}) fusion(f32[12,561,561]{1,2,0:T(8,128)} %get-tuple-element.166, f32[12,561]{1,0:T(8,128)S(1)} %copy-done.31, bf16[561,12,64]{0,2,1:T(8,128)(2,1)S(1)} %bitcast.404, bf16[561,12,64]{0,2,1:T(8,128)(2,1)S(1)} %bitcast.402), kind=kOutput, calls=%fused_computation.9 | convolution fusion | flops 494734656 | bytes 31990464 | tf_op jit(solution)/shard_map/ihd,jhd->hij/dot_general | solution.py:119
  380.8 12.1 %multiply_convert_fusion = bf16[12,561,561]{1,2,0:T(8,128)(2,1)S(1)} fusion(f32[12,561,561]{1,2,0:T(8,128)} %get-tuple-element.171, f32[12,561,561]{1,2,0:T(8,128)} %get-tuple-element.166, f32[12,561]{1,0:T(8,128)S(1)} %get-tuple-element.170, f32[12,561]{1,0:T(8,128)S(1)} %copy-done.31), kind=kLoop, calls=%fused_computation.8 | loop fusion | flops 15106608 | bytes 37820376 | tf_op jit(solution)/shard_map/convert_element_type | solution.py:121
  413.1 7.0 convert_bitcast_fusion
  440.1 7.7 %multiply_reduce_fusion.11 = (f32[768]{0:T(1024)S(1)}, f32[768]{0:T(1024)S(1)}, f32[768]{0:T(1024)S(1)}, f32[768]{0:T(1024)S(1)}, f32[768]{0:T(1024)S(1)}, /*ind...) fusion(f32[1,512,768]{2,1,0:T(8,128)} %slice.322, ...), kind=kLoop, calls=%fused_computation.154 | loop fusion | flops 7858176 | bytes 12622848 | tf_op jit(solution)/shard_map/transpose(jvp())/reduce_sum | solution.py:66
  458.5 44.4 %share_pages.1 = (bf16[4,561,768]{2,1,0:T(8,128)(2,1)}, bf16[4,561,768]{2,1,0:T(8,128)(2,1)}) custom-call(bf16[561,768]{1,0:T(8,128)(2,1)} %get-tuple-element.114.refs_0_, bf16[561,768]{1,0:T(8,128)(2,1)} %fusion.79.refs_1_), custom_call_target="tpu_custom_call" | custom-call | tf_op jit(solution)/shard_map/share_pages/pallas_call | solution.py:589
  508.2 6.3 copy.194
  514.5 12.0 %fusion.22 = f32[3,12,256,561]{2,3,0,1:T(8,128)} fusion(bf16[12,561,561]{1,2,0:T(8,128)(2,1)S(1)} %bitcast.376, s32[3,561]{1,0:T(4,128)S(1)} %bitcast.416), kind=kOutput, calls=%fused_computation.28 | convolution fusion | flops 5801368576 | bytes 28240740 | tf_op jit(solution)/shard_map/cia,hij->chaj/dot_general | solution.py:131
  526.6 22.6 %fusion.5 = f32[3,12,256,256]{3,2,1,0:T(8,128)S(1)} fusion(f32[3,12,256,561]{2,3,0,1:T(8,128)} %fusion.22, s32[3,561]{1,0:T(4,128)S(1)} %bitcast.417), kind=kOutput, calls=%fused_computation.4 | convolution fusion | flops 15883211776 | bytes 30124620 | tf_op jit(solution)/shard_map/chaj,cjb->chab/dot_general | solution.py:132
  549.2 32.4 %fusion.99 = f32[3,128,12]{1,2,0:T(8,128)S(1)} fusion(s32[256,256]{1,0:T(8,128)S(1)} %copy-done.33, f32[3,12,256,256]{3,2,1,0:T(8,128)S(1)} %fusion.5), kind=kOutput, calls=%fused_computation.176 | convolution fusion | flops 3632267264 | bytes 9717760 | tf_op jit(solution)/shard_map/abk,chab->ckh/dot_general | solution.py:770
  582.9 127.0 %reduce_grads.1 = (f32[8,128]{1,0:T(8,128)}, f32[96,576]{1,0:T(8,128)}, f32[24,768]{1,0:T(8,128)}, f32[96,768]{1,0:T(8,128)}, f32[96,768]{1,0:T(8,128)}) custom-call(f32[4,8,8,128]{3,2,1,0:T(8,128)} %copy.229, bf16[4,8,96,576]{3,2,1,0:T(8,128)(2,1)} %bitcast.379, bf16[4,8,24,768]{3,2,1,0:T(8,128)(2,1)} %convolution_convert_fusion.2.refs_2_, ...), custom_call_target="tpu_custom_call" | custom-call | tf_op jit(solution)/shard_map/reduce_grads/pallas_call | solution.py:522
  (409 shorter events, 189.4 us)
Async XLA Ops:
  2.6 18.6 %copy-start.80 = (s32[49]{0:T(128)}, s32[49]{0:T(128)S(1)}, u32[]{:S(2)}) copy-start(s32[49]{0:T(128)S(1)} %fusion.141) | copy-start | bytes 592
  7.5 13.3 %copy-start.73 = (f32[561]{0:T(1024)}, f32[561]{0:T(1024)S(1)}, u32[]{:S(2)}) copy-start(f32[561]{0:T(1024)S(1)} %get-tuple-element.179) | copy-start | bytes 6736
  7.5 193.8 %copy-start.34 = (s32[1,3,561]{2,1,0:T(4,128)}, s32[1,3,561]{2,1,0:T(4,128)S(1)}, u32[]{:S(2)}) copy-start(s32[1,3,561]{2,1,0:T(4,128)S(1)} %copy.230) | copy-start | bytes 20200
  21.2 128.0 %copy-start.8 = (f32[1,561,768]{2,1,0:T(8,128)}, f32[1,561,768]{2,1,0:T(8,128)S(1)}, u32[]{:S(2)}) copy-start(f32[1,561,768]{2,1,0:T(8,128)S(1)} %convert_multiply_fusion.1) | copy-start | bytes 5170180
  121.4 167.5 %copy-start.39 = (f32[768]{0:T(1024)}, f32[768]{0:T(1024)S(1)}, u32[]{:S(2)}) copy-start(f32[768]{0:T(1024)S(1)} %mul.710) | copy-start | bytes 9220
  149.4 15.3 %copy-start.45 = (f32[768]{0:T(1024)}, f32[768]{0:T(1024)S(1)}, u32[]{:S(2)}) copy-start(f32[768]{0:T(1024)S(1)} %mul.650) | copy-start | bytes 9220
  157.7 14.3 %copy-start.41 = (f32[768]{0:T(1024)}, f32[768]{0:T(1024)S(1)}, u32[]{:S(2)}) copy-start(f32[768]{0:T(1024)S(1)} %mul.676) | copy-start | bytes 9220
  172.0 85.6 %copy-start.5 = (f32[1,561,768]{2,1,0:T(8,128)}, f32[1,561,768]{2,1,0:T(8,128)S(1)}, u32[]{:S(2)}) copy-start(f32[1,561,768]{2,1,0:T(8,128)S(1)} %convert_add_fusion) | copy-start | bytes 5170180
  179.0 42.0 %copy-start.12 = (bf16[4,561,192]{1,2,0:T(8,128)(2,1)}, bf16[4,561,192]{1,2,0:T(8,128)(2,1)S(1)}, u32[]{:S(2)}) copy-start(bf16[4,561,192]{1,2,0:T(8,128)(2,1)S(1)} %copy.147) | copy-start | bytes 2585092
  201.3 19.7 %copy-start.82 = (pred[561]{0:T(1024)(128)(4,1)S(1)}, pred[561]{0:T(1024)(128)(4,1)}, u32[]{:S(2)}) copy-start(pred[561]{0:T(1024)(128)(4,1)} %get-tuple-element.178) | copy-start | bytes 1687
  257.5 22.0 %copy-start.71 = (f32[561]{0:T(1024)}, f32[561]{0:T(1024)S(1)}, u32[]{:S(2)}) copy-start(f32[561]{0:T(1024)S(1)} %multiply_reduce_fusion.4) | copy-start | bytes 6736
  296.6 13.6 %slice-start.3 = ((s8[6979584]{0:T(1024)(128)(4,1)}), s8[4194304]{0:T(1024)(128)(4,1)S(1)}, s32[]{:S(2)}) async-start(s8[6979584]{0:T(1024)(128)(4,1)} %bitcast.377), calls=%async_computation.3 | async-start | bytes 8388608
  296.6 29.9 %slice-start.5 = ((s8[4718592]{0:T(1024)(128)(4,1)}), s8[4194304]{0:T(1024)(128)(4,1)S(1)}, s32[]{:S(2)}) async-start(s8[4718592]{0:T(1024)(128)(4,1)} %bitcast.426), calls=%async_computation.5 | async-start | bytes 8388608
  299.3 27.2 %slice-start.6 = ((s8[4718592]{0:T(1024)(128)(4,1)}), s8[524288]{0:T(1024)(128)(4,1)S(1)}, s32[]{:S(2)}) async-start(s8[4718592]{0:T(1024)(128)(4,1)} %bitcast.426), calls=%async_computation.6 | async-start | bytes 1048576
  331.9 23.3 %copy-start.16 = (f32[561,768]{1,0:T(8,128)}, f32[561,768]{1,0:T(8,128)S(1)}, u32[]{:S(2)}) copy-start(f32[561,768]{1,0:T(8,128)S(1)} %get-tuple-element.104) | copy-start | bytes 5170180
  337.7 17.6 %copy-start.75 = (f32[561]{0:T(1024)}, f32[561]{0:T(1024)S(1)}, u32[]{:S(2)}) copy-start(f32[561]{0:T(1024)S(1)} %negate_multiply_fusion.1) | copy-start | bytes 6736
  380.8 12.2 %copy-start.14 = (bf16[4,561,192]{1,2,0:T(8,128)(2,1)S(1)}, bf16[4,561,192]{1,2,0:T(8,128)(2,1)}, u32[]{:S(2)}) copy-start(bf16[4,561,192]{1,2,0:T(8,128)(2,1)} %copy.146) | copy-start | bytes 2585092
  440.1 11.6 %copy-start.38 = (f32[1,8,4,24]{3,2,1,0:T(4,128)S(1)}, f32[1,8,4,24]{3,2,1,0:T(4,128)}, u32[]{:S(2)}) copy-start(f32[1,8,4,24]{3,2,1,0:T(4,128)} %stack.43) | copy-start | bytes 9220
  440.1 11.6 %copy-start.37 = (f32[1,8,4,24]{3,2,1,0:T(4,128)S(1)}, f32[1,8,4,24]{3,2,1,0:T(4,128)}, u32[]{:S(2)}) copy-start(f32[1,8,4,24]{3,2,1,0:T(4,128)} %stack.44) | copy-start | bytes 9220
  503.0 11.5 %slice-start = ((s8[8724480]{0:T(1024)(128)(4,1)}), s8[4194304]{0:T(1024)(128)(4,1)S(1)}, s32[]{:S(2)}) async-start(s8[8724480]{0:T(1024)(128)(4,1)} %bitcast.375), calls=%async_computation | async-start | bytes 8388608
  503.0 11.5 %slice-start.1 = ((s8[8724480]{0:T(1024)(128)(4,1)}), s8[4194304]{0:T(1024)(128)(4,1)S(1)}, s32[]{:S(2)}) async-start(s8[8724480]{0:T(1024)(128)(4,1)} %bitcast.375), calls=%async_computation.1 | async-start | bytes 8388608
  526.6 22.6 %copy-start.33 = (s32[256,256]{1,0:T(8,128)S(1)}, s32[256,256]{1,0:T(8,128)}, u32[]{:S(2)}) copy-start(s32[256,256]{1,0:T(8,128)} %clamp_add_fusion) | copy-start | bytes 786436
  549.2 32.9 %copy-start.36 = (f32[4,8,96]{2,1,0:T(8,128)S(1)}, f32[4,8,96]{2,1,0:T(8,128)}, u32[]{:S(2)}) copy-start(f32[4,8,96]{2,1,0:T(8,128)} %reshape.1045) | copy-start | bytes 36868
  582.9 140.7 %copy-start.1 = (s32[4,3,561]{2,0,1:T(4,128)S(1)}, s32[4,3,561]{2,0,1:T(4,128)}, u32[]{:S(2)}) copy-start(s32[4,3,561]{2,0,1:T(4,128)} %param.18) | copy-start | bytes 80788
  (71 other events, 369.4 us)
